TPU v7x, 256 devices: a whole 4x4x8 slice. The times are simulated.
256 devices in a mesh: prow: 16 (over y_hi, z), pcol: 16 (over x, y_lo, core).
Axes of the slice: x: 4, y: 4 (y_hi: 2, y_lo: 2; y = y_hi * 2 + y_lo), z: 8, core: 2. Of those that a mesh axis runs over, the one named last changes fastest.
Arguments:
- a_panel: float32 [98304, 512], P('prow', 'pcol'), may hold values from -6 to 6
- u_rows: float32 [512, 98304], P('pcol', 'prow'), may hold values from -0.25 to 0.25
- u_col: float32 [98304, 2048], P('prow', 'pcol'), may hold values from -0.01953125 to 0.01953125
- c_in: float32 [98304, 2048], P('prow', 'pcol'), may hold values from -6 to 6
Outputs:
- c_out: float32 [98304, 2048], P('prow', 'pcol')
All inputs are finite; a program needn't handle non-finite values.
Results may differ from a plain program's by a relative error of at most 0.00007.
Values sent between devices are 32-bit elements; how exact they have to be, the bound alone decides.
No kernel may reach another device: no remote copies, remote signals or barrier semaphores. Data moves between devices by JAX's collectives and lax.ppermute only.
A program may use at most 128 MiB of HBM per device.

v0:
```python
import jax
import jax.numpy as jnp
from jax import lax
from jax.sharding import PartitionSpec as P


def cut_along(x, dim, devices):
    before, after = (x.shape[:dim], x.shape[dim + 1 :])
    return jnp.moveaxis(x.reshape(*before, devices, -1, *after), dim, 0)


def summed_on_arrival(x, axis, dim):
    devices = lax.axis_size(axis)
    tiles = lax.all_to_all(cut_along(x, dim, devices), axis, 0, 0, tiled=True)
    return jnp.sum(tiles, axis=0)


def laid_out(tiles, dim):
    tiles = jnp.moveaxis(tiles, 0, dim)
    lengths = tiles.shape
    return tiles.reshape(*lengths[:dim], lengths[dim] * lengths[dim + 1], *lengths[dim + 2 :])


def sent_to_all(x, axis):
    copies = jnp.broadcast_to(x, (lax.axis_size(axis), *x.shape))
    return lax.all_to_all(copies, axis, split_axis=0, concat_axis=0, tiled=True)


def gather_directly(x, axis, dim):
    return laid_out(sent_to_all(x, axis), dim)


def on_device(a_panel, u_rows, u_col, c_in):
    a_full, u_full = (
        lax.all_gather(a_panel, "pcol", axis=1, tiled=True),
        lax.all_gather(u_rows, "pcol", axis=0, tiled=True),
    )
    inner_share = summed_on_arrival(
        jnp.dot(
            a_full.T, u_col, precision=lax.Precision.HIGHEST, preferred_element_type=jnp.float32
        ),
        "prow",
        0,
    )
    return c_in + jnp.dot(
        u_full.T,
        gather_directly(inner_share, "prow", 0),
        precision=lax.Precision.HIGHEST,
        preferred_element_type=jnp.float32,
    )


def solution(mesh):
    placed = (P("prow", "pcol"), P("pcol", "prow"), P("prow", "pcol"), P("prow", "pcol"))
    return jax.shard_map(
        on_device, mesh=mesh, in_specs=placed, out_specs=P("prow", "pcol"), check_vma=False
    )
```

profile of v0, /device:TPU:1, one launch (start us, length us, event | category | flops | bytes accessed | tf_op | source)
XLA Modules:
  0.0 193.7 jit_solution(4302002737189575478)
XLA Ops:
  6.5 0.0 copy-start
  6.5 0.0 all-gather.3.cloned.1.call-start
  6.5 0.7 all-gather.3.cloned.1.call-update
  7.3 0.0 all-gather.5.cloned.1.call-start
  7.3 0.7 all-gather.5.cloned.1.call-update
  8.0 79.7 %all-gather.3.cloned.1.call-done = f32[6144,512]{0,1:T(8,128)} async-done(((f32[6144,32]{0,1:T(8,128)}), f32[6144,512]{0,1:T(8,128)}) %all-gather.3.cloned.1.call-update) | async-done | bytes 12582928 | tf_op jit(solution)/shard_map/all_gather | solution.py:35
  87.8 0.0 copy-done
  87.8 12.5 %fusion.1 = f32[512,128]{1,0:T(8,128)S(1)} fusion(f32[6144,512]{0,1:T(8,128)} %all-gather.3.cloned.1.call-done, f32[6144,128]{1,0:T(8,128)S(1)} %copy-done), kind=kOutput, calls=%fused_computation.2 | convolution fusion | flops 4831838208 | bytes 15990784 | tf_op jit(solution)/shard_map/dot_general | solution.py:39
  100.2 19.5 %all_to_all.10 = f32[16,32,128]{2,1,0:T(8,128)S(1)} all-to-all(f32[16,32,128]{2,1,0:T(8,128)S(1)} %bitcast.11), channel_id=1, replica_groups=mesh['prow'=16,'pcol'=16] {'prow'}, dimensions={0} | all-to-all | bytes 524288 | tf_op jit(solution)/shard_map/all_to_all | solution.py:14
  119.7 0.7 broadcast_in_dim.3
  120.5 5.4 %all-to-all-start.1 = ((f32[16,32,128]{2,1,0:T(8,128)}), f32[16,32,128]{2,1,0:T(8,128)S(1)}, u32[]{:S(2)}, u32[]{:S(2)}) async-start(f32[16,32,128]{2,1,0:T(8,128)} %broadcast_in_dim.3), calls=%async_computation.1 | async-start | bytes 524288 | tf_op jit(solution)/shard_map/all_to_all | solution.py:26
  125.9 3.6 %copy.5 = f32[6144,128]{0,1:T(8,128)} copy(f32[6144,128]{1,0:T(8,128)} %param.7) | data formatting | bytes 6291456 | tf_op args[3]
  129.5 41.0 %all-gather.5.cloned.1.call-done = f32[512,6144]{1,0:T(8,128)} async-done(((f32[32,6144]{1,0:T(8,128)}), f32[512,6144]{1,0:T(8,128)}) %all-gather.5.cloned.1.call-update) | async-done | bytes 12582928 | tf_op jit(solution)/shard_map/all_gather | solution.py:36
  170.4 0.0 all-to-all-done.1
  170.5 12.9 %fusion = f32[6144,128]{0,1:T(8,128)} fusion(f32[6144,128]{0,1:T(8,128)} %copy.5, f32[512,128]{1,0:T(8,128)S(1)} %bitcast.10, f32[512,6144]{1,0:T(8,128)} %all-gather.5.cloned.1.call-done), kind=kOutput, calls=%fused_computation.1 | convolution fusion | flops 4832624640 | bytes 19136512 | tf_op jit(solution)/shard_map/dot_general | solution.py:45
  183.3 3.5 %copy.6 = f32[6144,128]{1,0:T(8,128)} copy(f32[6144,128]{0,1:T(8,128)} %fusion) | data formatting | bytes 6291456 | tf_op jit(solution)/shard_map/add | solution.py:45
  (1 shorter events, 0.0 us)
Async XLA Ops:
  6.5 81.2 %copy-start = (f32[6144,128]{1,0:T(8,128)S(1)}, f32[6144,128]{1,0:T(8,128)}, u32[]{:S(2)}) copy-start(f32[6144,128]{1,0:T(8,128)} %param.6) | copy-start | bytes 9437188
  6.5 81.2 %all-gather.3.cloned.1.call-start = ((), (), s32[]{:S(2)}) async-start(), calls=%async_computation.2 | async-start | bytes 13369344 | tf_op jit(solution)/shard_map/all_gather | solution.py:35
  7.3 163.2 %all-gather.5.cloned.1.call-start = ((), (), s32[]{:S(2)}) async-start(), calls=%async_computation.3 | async-start | bytes 13369344 | tf_op jit(solution)/shard_map/all_gather | solution.py:36
  120.5 50.0 %all-to-all-start.1 = ((f32[16,32,128]{2,1,0:T(8,128)}), f32[16,32,128]{2,1,0:T(8,128)S(1)}, u32[]{:S(2)}, u32[]{:S(2)}) async-start(f32[16,32,128]{2,1,0:T(8,128)} %broadcast_in_dim.3), calls=%async_computation.1 | async-start | bytes 524288 | tf_op jit(solution)/shard_map/all_to_all | solution.py:26
Sparse Core Ops, SparseCore 0:
  9.2 78.5 all-gather.2
  89.6 80.8 all-gather.4
where the time goes:
time: 194 us
  waiting for transfers between devices  122 us (63%)
  matrix products  25.3 us (13%)
  blocking collectives  19.5 us (10%)
  between operations  13.4 us (7%)
  local copies, waits for them, and re-layouts  7.86 us (4%)
  starting transfers between devices  5.45 us (3%)
    all_gather x1, waiting for transfers between devices, on_device(): lax.all_gather(a_panel, 'pcol', axis=1, tiled=True)  79.7 us
    all_gather x1, waiting for transfers between devices, on_device(): lax.all_gather(u_rows, 'pcol', axis=0, tiled=True)  41 us
    all_to_all x1, blocking collectives, summed_on_arrival(): tiles = lax.all_to_all(cut_along(x, dim, devices), axis, 0, 0, tiled=True)  19.5 us
    dot_general x1, matrix products, on_device(): jnp.dot(u_full.T, gather_directly(inner_share, 'prow', 0), precision=lax....  12.9 us
    dot_general x1, matrix products, on_device(): jnp.dot(a_full.T, u_col, precision=lax.Precision.HIGHEST, preferred_eleme...  12.5 us
    all_to_all x1, starting transfers between devices, sent_to_all(): return lax.all_to_all(copies, axis, split_axis=0, concat_axis=0, tiled=True)  5.41 us
  transfers between devices with their start and end apart: 3, of which 2 were waited for; matrix products, arithmetic and copies ran while one was open for 9% of the time, Pallas kernels for 0%

commit v1 on v0

--- a/solution.py
+++ b/solution.py
@@ -33,7 +33,9 @@
 def on_device(a_panel, u_rows, u_col, c_in):
     a_full, u_full = (
         lax.all_gather(a_panel, "pcol", axis=1, tiled=True),
-        lax.all_gather(u_rows, "pcol", axis=0, tiled=True),
+        jnp.concatenate(
+            lax.all_to_all(jnp.stack([u_rows] * lax.axis_size("pcol")), "pcol", 0, 0), axis=0
+        ),
     )
     inner_share = summed_on_arrival(
         jnp.dot(

time: 194 us -> 375 us (1.93)
  waiting for transfers between devices: 122 us -> 290 us
  local copies, waits for them, and re-layouts: 7.86 us -> 13.8 us
  starting transfers between devices: 5.45 us -> 10.8 us
    all_to_all x0 -> x1, waiting for transfers between devices: none -> 202 us  [on_device(): lax.all_to_all(jnp.stack([u_rows] * lax.axis_size('pcol')), 'pcol', 0, 0)]
    all_gather x1 -> x0, waiting for transfers between devices: 41 us -> none  [on_device(): lax.all_gather(u_rows, 'pcol', axis=0, tiled=True)]
    all_to_all x0 -> x1, starting transfers between devices: none -> 6.78 us  [on_device(): lax.all_to_all(jnp.stack([u_rows] * lax.axis_size('pcol')), 'pcol', 0, 0)]
    all_to_all x1, waiting for transfers between devices: 0.01 us -> 6.74 us  [sent_to_all(): return lax.all_to_all(copies, axis, split_axis=0, concat_axis=0, tiled=True)]
    another operation x0 -> x1, local copies, waits for them, and re-layouts: none -> 5.99 us  [on_device(): jnp.stack([u_rows] * lax.axis_size('pcol'))]
  transfers between devices with their start and end apart: 3 -> 3, of which waited for: 2 -> 3; matrix products, arithmetic and copies ran while one was open for 9% -> 1% of each run, Pallas kernels for 0% -> 0%
where the time goes in v1:
time: 375 us; the launch traced here: 373 us
  waiting for transfers between devices  290 us (77%)
  matrix products  25.4 us (7%)
  blocking collectives  19.5 us (5%)
  local copies, waits for them, and re-layouts  13.8 us (4%)
  between operations  13.4 us (4%)
  starting transfers between devices  10.8 us (3%)
    all_to_all x1, waiting for transfers between devices, on_device(): lax.all_to_all(jnp.stack([u_rows] * lax.axis_size('pcol')), 'pcol', 0, 0)  202 us
    all_gather x1, waiting for transfers between devices, on_device(): lax.all_gather(a_panel, 'pcol', axis=1, tiled=True)  80.5 us
    all_to_all x1, blocking collectives, summed_on_arrival(): tiles = lax.all_to_all(cut_along(x, dim, devices), axis, 0, 0, tiled=True)  19.5 us
    dot_general x1, matrix products, on_device(): jnp.dot(u_full.T, gather_directly(inner_share, 'prow', 0), precision=lax....  12.9 us
    dot_general x1, matrix products, on_device(): jnp.dot(a_full.T, u_col, precision=lax.Precision.HIGHEST, preferred_eleme...  12.6 us
  transfers between devices with their start and end apart: 3, of which 3 were waited for; matrix products, arithmetic and copies ran while one was open for 1% of the time, Pallas kernels for 0%

profile of v1, /device:TPU:1, one launch (start us, length us, event | category | flops | bytes accessed | tf_op | source)
XLA Modules:
  0.0 373.0 jit_solution(992965104362783421)
XLA Ops:
  6.5 0.0 copy-start
  6.5 0.0 all-gather.2.cloned.1.call-start
  6.5 0.7 all-gather.2.cloned.1.call-update
  7.3 80.5 %all-gather.2.cloned.1.call-done = f32[6144,512]{0,1:T(8,128)} async-done(((f32[6144,32]{0,1:T(8,128)}), f32[6144,512]{0,1:T(8,128)}) %all-gather.2.cloned.1.call-update) | async-done | bytes 12582928 | tf_op jit(solution)/shard_map/all_gather | solution.py:35
  87.8 0.0 copy-done
  87.8 0.0 copy-start.1
  87.8 12.6 %fusion.1 = f32[512,128]{1,0:T(8,128)S(1)} fusion(f32[6144,512]{0,1:T(8,128)} %all-gather.2.cloned.1.call-done, f32[6144,128]{1,0:T(8,128)S(1)} %copy-done), kind=kOutput, calls=%fused_computation.2 | convolution fusion | flops 4831838208 | bytes 15990784 | tf_op jit(solution)/shard_map/dot_general | solution.py:41
  100.3 19.5 %all_to_all.15 = f32[16,32,128]{2,1,0:T(8,128)S(1)} all-to-all(f32[16,32,128]{2,1,0:T(8,128)S(1)} %bitcast.11), channel_id=1, replica_groups=mesh['prow'=16,'pcol'=16] {'prow'}, dimensions={0} | all-to-all | bytes 524288 | tf_op jit(solution)/shard_map/all_to_all | solution.py:14
  119.8 0.0 copy-done.1
  119.8 6.0 %stack.2 = f32[16,32,6144]{2,1,0:T(8,128)} broadcast(f32[32,6144]{1,0:T(8,128)S(1)} %copy-done.1), dimensions={1,2} | broadcast | bytes 13369344 | tf_op jit(solution)/shard_map/stack | solution.py:37
  125.8 6.8 %all-to-all-start.2 = ((f32[16,32,6144]{2,1,0:T(8,128)}), f32[16,32,6144]{2,1,0:T(8,128)}, u32[]{:S(2)}, u32[]{:S(2)}) async-start(f32[16,32,6144]{2,1,0:T(8,128)} %stack.2), calls=%async_computation.2 | async-start | bytes 25165824 | tf_op jit(solution)/shard_map/all_to_all | solution.py:37
  132.6 202.1 %all-to-all-done.2 = f32[16,32,6144]{2,1,0:T(8,128)} async-done(((f32[16,32,6144]{2,1,0:T(8,128)}), f32[16,32,6144]{2,1,0:T(8,128)}, u32[]{:S(2)}, u32[]{:S(2)}) %all-to-all-start.2) | async-done | bytes 12582944 | tf_op jit(solution)/shard_map/all_to_all | solution.py:37
  334.7 0.7 broadcast_in_dim.3
  335.4 4.0 %all-to-all-start.1 = ((f32[16,32,128]{2,1,0:T(8,128)}), f32[16,32,128]{2,1,0:T(8,128)S(1)}, u32[]{:S(2)}, u32[]{:S(2)}) async-start(f32[16,32,128]{2,1,0:T(8,128)} %broadcast_in_dim.3), calls=%async_computation.1 | async-start | bytes 524288 | tf_op jit(solution)/shard_map/all_to_all | solution.py:26
  339.4 3.5 copy.5
  343.0 6.7 %all-to-all-done.1 = f32[16,32,128]{2,1,0:T(8,128)S(1)} async-done(((f32[16,32,128]{2,1,0:T(8,128)}), f32[16,32,128]{2,1,0:T(8,128)S(1)}, u32[]{:S(2)}, u32[]{:S(2)}) %all-to-all-start.1) | async-done | bytes 262176 | tf_op jit(solution)/shard_map/all_to_all | solution.py:26
  349.7 12.9 %fusion = f32[6144,128]{0,1:T(8,128)} fusion(f32[6144,128]{0,1:T(8,128)} %copy.5, f32[16,32,128]{2,1,0:T(8,128)S(1)} %all-to-all-done.1, f32[16,32,6144]{2,1,0:T(8,128)} %all-to-all-done.2), kind=kOutput, calls=%fused_computation.1 | convolution fusion | flops 4832624640 | bytes 19136512 | tf_op jit(solution)/shard_map/dot_general | solution.py:47
  362.6 3.5 copy.6
  (1 shorter events, 0.0 us)
Async XLA Ops:
  6.5 81.2 %copy-start = (f32[6144,128]{1,0:T(8,128)S(1)}, f32[6144,128]{1,0:T(8,128)}, u32[]{:S(2)}) copy-start(f32[6144,128]{1,0:T(8,128)} %param.6) | copy-start | bytes 9437188
  6.5 81.2 %all-gather.2.cloned.1.call-start = ((), (), s32[]{:S(2)}) async-start(), calls=%async_computation.3 | async-start | bytes 13369344 | tf_op jit(solution)/shard_map/all_gather | solution.py:35
  87.8 32.0 %copy-start.1 = (f32[32,6144]{1,0:T(8,128)S(1)}, f32[32,6144]{1,0:T(8,128)}, u32[]{:S(2)}) copy-start(f32[32,6144]{1,0:T(8,128)} %param.5) | copy-start | bytes 2359300
  125.8 208.9 %all-to-all-start.2 = ((f32[16,32,6144]{2,1,0:T(8,128)}), f32[16,32,6144]{2,1,0:T(8,128)}, u32[]{:S(2)}, u32[]{:S(2)}) async-start(f32[16,32,6144]{2,1,0:T(8,128)} %stack.2), calls=%async_computation.2 | async-start | bytes 25165824 | tf_op jit(solution)/shard_map/all_to_all | solution.py:37
  335.4 14.3 %all-to-all-start.1 = ((f32[16,32,128]{2,1,0:T(8,128)}), f32[16,32,128]{2,1,0:T(8,128)S(1)}, u32[]{:S(2)}, u32[]{:S(2)}) async-start(f32[16,32,128]{2,1,0:T(8,128)} %broadcast_in_dim.3), calls=%async_computation.1 | async-start | bytes 524288 | tf_op jit(solution)/shard_map/all_to_all | solution.py:26
Sparse Core Ops, SparseCore 0:
  9.2 78.5 all-gather.1
